TPU v7x, 256 devices: a whole 4x4x8 slice. The times are simulated.
256 devices in a mesh: row: 16 (over x, z_lo, core), col: 16 (over z_hi, y).
Axes of the slice: x: 4, y: 4, z: 8 (z_hi: 4, z_lo: 2; z = z_hi * 2 + z_lo), core: 2. Of those that a mesh axis runs over, the one named last changes fastest.
Arguments:
- first_set: float32 [16384, 128], P(('row', 'col')), may hold values from -64 to 64, as said below
- second_set: float32 [16384, 128], P(('row', 'col')), may hold values from -64 to 64, as said below
- query_weight: float32 [2, 128, 128], replicated, may hold values from -0.5 to 0.5
- key_weight: float32 [2, 128, 128], replicated, may hold values from -0.5 to 0.5
- norm_gain: float32 [2, 128], replicated, may hold values from 0.25 to 1.75
- up_weight: float32 [2, 128, 512], replicated, may hold values from -0.5 to 0.5
- up_bias: float32 [2, 512], replicated, may hold values from -3 to 3
- down_weight: float32 [2, 512, 128], replicated, may hold values from -0.25 to 0.25
Outputs:
- first_out: float32 [16384, 128], P(('row', 'col'))
- second_out: float32 [16384, 128], P(('row', 'col'))
Inputs may be any that keep to these rules, and one draw needn't show every extreme that they name: `first_set`: rows have differing scales. `second_set`: rows have differing scales.
All inputs are finite; a program needn't handle non-finite values.
Results may differ from a plain program's by a relative error of at most 0.0004.
Values sent between devices are 32-bit elements; how exact they have to be, the bound alone decides.
A program may use at most 64 MiB of HBM per device.

v0:
```python
import functools
import math

import jax
import jax.numpy as jnp
from jax import lax
from jax.experimental import pallas as pl
from jax.experimental.pallas import tpu as pltpu
from jax.sharding import PartitionSpec as P

MESH = pl.DeviceIdType.MESH
F32, BF16 = jnp.float32, jnp.bfloat16
HIGH = lax.Precision.HIGHEST
LOG2E = math.log2(math.e)
NT = (((1,), (1,)), ((), ()))


def dot(a, b, dims=(((1,), (0,)), ((), ()))):
    return lax.dot_general(a, b, dims, preferred_element_type=F32)


def high(a, b, dims=(((1,), (0,)), ((), ()))):
    return lax.dot_general(a, b, dims, precision=HIGH, preferred_element_type=F32)


def split2(v):
    top = v.astype(BF16)
    return top, (v - top.astype(F32)).astype(BF16)


def split3(v):
    top = v.astype(BF16)
    rest = v - top.astype(F32)
    mid = rest.astype(BF16)
    return top, mid, (rest - mid.astype(F32)).astype(BF16)


def eye(rows, shift=0):
    r = lax.broadcasted_iota(jnp.int32, (rows, 128), 0)
    c = lax.broadcasted_iota(jnp.int32, (rows, 128), 1)
    return c == r + shift


def to_lanes(column, mask):
    spread = jnp.broadcast_to(column, mask.shape)
    return jnp.sum(jnp.where(mask, spread, 0.0), axis=0, keepdims=True)


def to_rows(line, mask):
    spread = jnp.broadcast_to(line, mask.shape)
    return jnp.sum(jnp.where(mask, spread, 0.0), axis=1, keepdims=True)


def kernel(
    dims, total, x_ref, y_ref, wq, wk, gain, up, bias, down, o1, o2,
    A, B, S, MH, ML, T1, T2, K1, K2, K3, AT, BC, RM, RS, RB, RW,
    rsend, csend, rgot, cgot, PS, PR, QS, QX, QR,
    sa, ra_, sb, rb_, sf, rf, ssr, rsr, ssc, rsc, sp, rp, sx, rx, sq, rq,
):
    nx, ny, nz = dims
    ga, gb = nx * ny, nz * 2
    row, col = lax.axis_index("row"), lax.axis_index("col")
    x, zl, k = lax.div(row, 4), lax.rem(lax.div(row, 2), 2), lax.rem(row, 2)
    zh, y = lax.div(col, ny), lax.rem(col, ny)
    z = zh * 2 + zl
    me_a, me_b = x * ny + y, z * 2 + k
    blk = x_ref.shape[0]
    rows, cols = ga * blk, gb * blk
    rchunk, cchunk = min(256, rows), min(256, cols)
    offset = 0.05 / total
    factor = 2.0 / math.sqrt(x_ref.shape[1]) * LOG2E
    pad = PS.shape[1]

    def at(x, y, z, k):
        return (x * 4 + lax.rem(z, 2) * 2 + k, lax.div(z, 2) * ny + y)

    def plane(n):
        dx, dy = n
        px, py = lax.rem(x + dx, nx), lax.rem(y + dy, ny)
        return px * ny + py, at(px, py, z, k)

    def line(dz, other):
        pz = lax.rem(z + dz, nz)
        pk = 1 - k if other else k
        return pz * 2 + pk, at(x, y, pz, pk)

    near = lambda d, n: min(d, n - d)
    plane_steps = sorted(
        [(dx, dy) for dx in range(nx) for dy in range(ny) if (dx, dy) != (0, 0)],
        key=lambda s: -near(s[0], nx) - near(s[1], ny),
    )
    z_steps = sorted(range(1, nz), key=lambda d: near(d, nz))
    line_steps = [(d, o) for d in [*z_steps[::-1], 0] for o in (False, True) if (d, o) != (0, False)]

    def copy(src, dst, ss, rs, dev):
        return pltpu.make_async_remote_copy(
            src_ref=src, dst_ref=dst, send_sem=ss, recv_sem=rs, device_id=dev, device_id_type=MESH
        )

    barrier = pltpu.get_barrier_semaphore()
    for step in plane_steps:
        pl.semaphore_signal(barrier, inc=1, device_id=plane(step)[1], device_id_type=MESH)
    for step in line_steps:
        pl.semaphore_signal(barrier, inc=1, device_id=line(*step)[1], device_id_type=MESH)
    o1[...] = x_ref[...]
    o2[...] = y_ref[...]
    pl.semaphore_wait(barrier, len(plane_steps) + len(line_steps))

    def slot(n):
        return pl.ds(pl.multiple_of(n * blk, blk), blk)

    def layer(l, carry):
        A[l, slot(me_a), :] = o1[...]
        B[l, slot(me_b), :] = o2[...]
        sent = []

        def send(src, dst, ss, rs, dev):
            c = copy(src, dst, ss, rs, dev)
            c.start()
            sent.append(c)

        own_a, own_b = A.at[l, slot(me_a)], B.at[l, slot(me_b)]
        _, sibling = line(0, True)
        send(own_b, own_b, sb.at[l, nz - 1], rf.at[l, z], sibling)
        for n, d in enumerate(z_steps[::-1]):
            send(own_b, own_b, sb.at[l, n], rb_.at[l, z], line(d, False)[1])
        for n, step in enumerate(plane_steps):
            send(own_a, own_a, sa.at[l, n], ra_.at[l, me_a], plane(step)[1])

        mix = high(wk[l], wq[l], NT) * factor

        for n, d in enumerate(z_steps):
            s, dev = line(d, False)
            ref = B.at[l, slot(s)]
            pz = lax.rem(z + d, nz)
            copy(ref, ref, sf.at[l, n], rb_.at[l, pz], sibling).wait_recv()
            send(ref, ref, sf.at[l, n], rf.at[l, pz], sibling)
        for d in range(nz):
            s, dev = line(d, True)
            ref = B.at[l, slot(s)]
            copy(ref, ref, sf.at[l, 0], rf.at[l, lax.rem(z + d, nz)], sibling).wait_recv()

        def make_keys(n, c):
            at_ = pl.ds(pl.multiple_of(n * 128, 128), 128)
            v = B[l, at_, :]
            b1, b2 = split2(v)
            BC[at_, 0:128] = b1
            BC[at_, 128:256] = b2
            k1, k2, k3 = split3(high(v, mix))
            K1[at_, 0:128] = k1
            K1[at_, 128:256] = k2
            K2[at_, 0:128] = k2
            K2[at_, 128:256] = k1
            K3[at_, 0:128] = k3
            K3[at_, 128:256] = k1
            return c

        lax.fori_loop(0, cols // 128, make_keys, 0)

        for step in plane_steps[::-1]:
            s, dev = plane(step)
            ref = A.at[l, slot(s)]
            copy(ref, ref, sa.at[l, 0], ra_.at[l, s], dev).wait_recv()

        def make_rows(n, c):
            at_ = pl.ds(pl.multiple_of(n * 128, 128), 128)
            v = A[l, at_, :]
            a1, a2, a3 = split3(v)
            T1[at_, 0:128] = a1
            T1[at_, 128:256] = a2
            T2[at_, 0:128] = a1
            T2[at_, 128:256] = a3
            t1, t2 = split2(v.T)
            AT[0:128, at_] = t1
            AT[128:256, at_] = t2
            return c

        lax.fori_loop(0, rows // 128, make_rows, 0)

        def score(n, carry):
            cm, cs = carry
            at_ = pl.ds(pl.multiple_of(n * rchunk, rchunk), rchunk)
            t1, t2 = T1[at_, :], T2[at_, :]
            S[at_, :] = dot(t1, K1[...], NT) + dot(t1, K2[...], NT) + dot(t2, K3[...], NT)
            base = n * rchunk

            def peak(i, m):
                for u in range(4):
                    m = jnp.maximum(m, S[pl.ds(pl.multiple_of(base + i * 32 + u * 8, 8), 8), :])
                return m

            new = lax.fori_loop(0, rchunk // 32, peak, cm)
            cs = cs * jnp.exp2(cm - new)

            def sums(i, c):
                for u in range(4):
                    r = pl.ds(pl.multiple_of(base + i * 32 + u * 8, 8), 8)
                    s = S[r, :]
                    parts = [s[:, j * 128 : (j + 1) * 128] for j in range(cols // 128)]
                    m = functools.reduce(jnp.maximum, parts)
                    RM[r, :] = m
                    RS[r, :] = functools.reduce(jnp.add, [jnp.exp2(p - m) for p in parts])
                    c = c + jnp.exp2(s - new)
                return c

            return new, lax.fori_loop(0, rchunk // 32, sums, cs)

        cm, cs = lax.fori_loop(
            0, rows // rchunk, score,
            (jnp.full((8, cols), -jnp.inf, F32), jnp.zeros((8, cols), F32)),
        )
        cpeak = jnp.max(cm, axis=0, keepdims=True)
        clse = cpeak + jnp.log(jnp.sum(cs * jnp.exp2(cm - cpeak), axis=0, keepdims=True)) * LOG2E
        for j in range(cols // 128):
            csend[j : j + 1, :] = clse[:, j * 128 : (j + 1) * 128]
        same = eye(128)

        def row_lse(n, c):
            at_ = pl.ds(pl.multiple_of(n * 128, 128), 128)
            m = RM[at_, :]
            p = jnp.max(m, axis=1, keepdims=True)
            t = jnp.sum(RS[at_, :] * jnp.exp2(m - p), axis=1, keepdims=True)
            rsend[pl.ds(n, 1), :] = to_lanes(p + jnp.log(t) * LOG2E, same)
            return c

        for n, step in enumerate(line_steps):
            send(csend, cgot.at[l, me_b], ssc.at[l, n], rsc.at[l, me_b], line(*step)[1])
        lax.fori_loop(0, rows // 128, row_lse, 0)

        for n, step in enumerate(plane_steps):
            send(rsend, rgot.at[l, me_a], ssr.at[l, n], rsr.at[l, me_a], plane(step)[1])
        cgot[l, me_b] = csend[...]
        rgot[l, me_a] = rsend[...]
        for step in plane_steps[::-1]:
            s, dev = plane(step)
            copy(rsend, rgot.at[l, s], ssr.at[l, 0], rsr.at[l, s], dev).wait_recv()

        def lse(got):
            p = jnp.max(got, axis=0)
            return p + jnp.log(jnp.sum(jnp.exp2(got - p), axis=0)) * LOG2E

        rw = lse(rgot[l])
        RW[...] = rw

        def spread(n, c):
            at_ = pl.ds(pl.multiple_of(n * 128, 128), 128)
            RB[at_, :] = jnp.broadcast_to(to_rows(RW[pl.ds(n, 1), :], same), (128, 128))
            RM[at_, :] = jnp.zeros((128, 128), F32)
            return c

        lax.fori_loop(0, rows // 128, spread, 0)
        for step in line_steps[::-1]:
            s, dev = line(*step)
            copy(csend, cgot.at[l, s], ssc.at[l, 0], rsc.at[l, s], dev).wait_recv()
        RW[...] = lse(cgot[l])

        lanes = cchunk // 128
        per = cchunk // blk

        def columns(n, carry):
            at_ = pl.ds(pl.multiple_of(n * cchunk, cchunk), cchunk)
            c = jnp.concatenate([RW[pl.ds(n * lanes + j, 1), :] for j in range(lanes)], axis=1)
            cb = jnp.broadcast_to(c, (16, cchunk))

            def piece(i, mass):
                for u in range(4):
                    r = pl.ds(pl.multiple_of(i * 64 + u * 16, 16), 16)
                    s = S[r, at_]
                    rb = RB[r, :]
                    rb = jnp.concatenate([rb] * lanes, axis=1)
                    m = jnp.exp2((s - rb) + (s - cb))
                    RM[r, :] += functools.reduce(
                        jnp.add, [m[:, j * 128 : (j + 1) * 128] for j in range(lanes)]
                    )
                    mass = mass + (m[0:8] + m[8:16])
                    h, lo = split2(m)
                    MH[r, at_] = h
                    ML[r, at_] = lo
                return mass

            mass = lax.fori_loop(0, rows // 64, piece, jnp.zeros((8, cchunk), F32))
            mass = jnp.sum(mass, axis=0, keepdims=True)
            q = dot(AT[...], MH[:, at_])
            q = q[0:128] + q[128:256] + dot(AT[0:128, :], ML[:, at_])
            for j in range(lanes):
                t = q[:, j * 128 : (j + 1) * 128].T
                for b in range(128 // blk):
                    QS[n * per + j * (128 // blk) + b, 0:blk, :] = t[b * blk : (b + 1) * blk]
                    QS[n * per + j * (128 // blk) + b, blk:pad, :] = jnp.broadcast_to(
                        mass[:, j * 128 : (j + 1) * 128], (pad - blk, 128)
                    )
            for b in range(per // 2):
                zz = n * (per // 2) + b
                copy(
                    QS.at[zz * 2 + (1 - k)], QX.at[l, zz], sx.at[l, zz], rx.at[l, zz], sibling
                ).start()
            return carry

        lax.fori_loop(0, cols // cchunk, columns, 0)

        small = eye(blk)

        def messages(n, carry):
            at_ = pl.ds(pl.multiple_of(n * rchunk, rchunk), rchunk)
            p = dot(MH[at_, :], BC[...])
            p = p[:, 0:128] + p[:, 128:256] + dot(ML[at_, :], BC[:, 0:128])
            mass = jnp.sum(RM[at_, :], axis=1, keepdims=True)
            for b in range(rchunk // blk):
                PS[n * (rchunk // blk) + b, 0:blk, :] = p[b * blk : (b + 1) * blk]
                PS[n * (rchunk // blk) + b, blk:pad, :] = jnp.broadcast_to(
                    to_lanes(mass[b * blk : (b + 1) * blk], small), (pad - blk, 128)
                )
            return carry

        def forward(zz):
            copy(
                QS.at[zz * 2 + (1 - k)], QX.at[l, zz], sx.at[l, zz], rx.at[l, zz], sibling
            ).wait_recv()
            return QS[zz * 2 + k] + QX[l, zz]

        for n, d in enumerate(z_steps[::-1]):
            pz = lax.rem(z + d, nz)
            QS[pz * 2 + k] = forward(pz)
            send(QS.at[pz * 2 + k], QR.at[l, z], sq.at[l, n], rq.at[l, z], line(d, False)[1])
        QR[l, z] = forward(z)

        lax.fori_loop(0, rows // rchunk, messages, 0)
        for n, step in enumerate(plane_steps):
            s, dev = plane(step)
            send(PS.at[s], PR.at[l, me_a], sp.at[l, n], rp.at[l, me_a], dev)
        PR[l, me_a] = PS[me_a]

        for n, d in enumerate(z_steps):
            s, dev = line(d, False)
            pz = lax.rem(z + d, nz)
            copy(QS.at[0], QR.at[l, pz], sq.at[l, 0], rq.at[l, pz], dev).wait_recv()
        q = jnp.sum(QR[l], axis=0)
        for step in plane_steps[::-1]:
            s, dev = plane(step)
            copy(PS.at[0], PR.at[l, s], sp.at[l, 0], rp.at[l, s], dev).wait_recv()
        p = jnp.sum(PR[l], axis=0)
        pm = to_rows(p[blk : blk + 1], small)
        qm = to_rows(q[blk : blk + 1], eye(blk, lax.rem(me_b, 128 // blk) * blk))
        hx = o1[...] + p[0:blk] / (pm + offset)
        hy = o2[...] + q[0:blk] / (qm + offset)
        h = jnp.concatenate([hx, hy], axis=0)
        scale = lax.rsqrt(jnp.mean(h * h, axis=1, keepdims=True) + 1e-05)
        u = high(h * scale * gain[l], up[l]) + bias[l]
        g = 0.5 * u * (1.0 + jnp.tanh(math.sqrt(2 / math.pi) * (u + 0.044715 * (u * u * u))))
        h = h + high(g, down[l])
        o1[...] = h[0:blk]
        o2[...] = h[blk : 2 * blk]
        for c in sent:
            c.wait_send()
        for zz in range(nz):
            copy(QS.at[zz * 2 + (1 - k)], QX.at[l, zz], sx.at[l, zz], rx.at[l, zz], sibling).wait_send()
        return carry

    lax.fori_loop(0, 2, layer, 0)


def align_all(dims, x, y, wq, wk, gain, up, bias, down):
    nx, ny, nz = dims
    ga, gb = nx * ny, nz * 2
    blk, d = x.shape
    rows, cols = ga * blk, gb * blk
    L = wq.shape[0]
    pad = blk + 8
    V, dma = pltpu.VMEM, lambda *s: pltpu.SemaphoreType.DMA(s)
    body = functools.partial(kernel, dims, blk * ga * gb)
    return pl.pallas_call(
        body,
        out_shape=[jax.ShapeDtypeStruct((blk, d), F32)] * 2,
        in_specs=[pl.BlockSpec(memory_space=V)] * 8,
        out_specs=[pl.BlockSpec(memory_space=V)] * 2,
        scratch_shapes=[
            V((L, rows, d), F32), V((L, cols, d), F32), V((rows, cols), F32),
            V((rows, cols), BF16), V((rows, cols), BF16),
            V((rows, 2 * d), BF16), V((rows, 2 * d), BF16),
            V((cols, 2 * d), BF16), V((cols, 2 * d), BF16), V((cols, 2 * d), BF16),
            V((2 * d, rows), BF16), V((cols, 2 * d), BF16),
            V((rows, 128), F32), V((rows, 128), F32), V((rows, 128), F32),
            V((max(rows, cols) // 128, 128), F32),
            V((rows // 128, 128), F32), V((cols // 128, 128), F32),
            V((L, ga, rows // 128, 128), F32), V((L, gb, cols // 128, 128), F32),
            V((ga, pad, d), F32), V((L, ga, pad, d), F32),
            V((gb, pad, d), F32), V((L, nz, pad, d), F32), V((L, nz, pad, d), F32),
            dma(L, ga), dma(L, ga), dma(L, nz), dma(L, nz), dma(L, nz), dma(L, nz),
            dma(L, ga), dma(L, ga), dma(L, gb), dma(L, gb),
            dma(L, ga), dma(L, ga), dma(L, nz), dma(L, nz), dma(L, nz), dma(L, nz),
        ],
        compiler_params=pltpu.CompilerParams(
            collective_id=0, has_side_effects=True, vmem_limit_bytes=60 * 1024 * 1024
        ),
    )(x, y, wq, wk, gain[:, None, :], up, bias[:, None, :], down)


def solution(mesh):
    size = mesh.shape["row"] * mesh.shape["col"]
    dims = (4, 4, 8) if size == 256 else (2, 2, 2)
    placed = (P(("row", "col"), None), P(("row", "col"), None), P(), P(), P(), P(), P(), P())
    return jax.shard_map(
        functools.partial(align_all, dims),
        mesh=mesh,
        in_specs=placed,
        out_specs=(P(("row", "col"), None), P(("row", "col"), None)),
        check_vma=False,
    )
```

profile of v0, /device:TPU:1, one launch (start us, length us, event | category | flops | bytes accessed | tf_op | source)
XLA Modules:
  0.0 98.6 jit_solution(11896114336490141136)
XLA Ops:
  0.6 1.3 %broadcast_in_dim.7.bias = f32[2,1,512]{2,1,0:T(1,128)} reshape(f32[2,512]{1,0:T(2,128)} %param.14) | data formatting | bytes 8192 | tf_op jit(solution)/shard_map/broadcast_in_dim | solution.py:395
  1.9 94.7 %shard_map.95 = (f32[64,128]{1,0:T(8,128)}, f32[64,128]{1,0:T(8,128)}) custom-call(f32[64,128]{1,0:T(8,128)} %x_ref.1, f32[64,128]{1,0:T(8,128)} %y_ref.1, f32[2,128,128]{2,1,0:T(8,128)} %wq.1, f32[2,128,128]{2,1,0:T(8,128)} %wk.1, f32[2,1,128]{2,1,0:T(1,128)} %bitcast.1, f32[2,128,512]{2,1,0:T(8,128)} %up.1, f32[2,1,512]{2,1,0:T(1,128)} %broadcast_in_dim.7.bias, ...), custom_call_target="tpu_custom_call" | custom-call | tf_op jit(solution)/shard_map/pallas_call | solution.py:371
  96.6 0.0 copy-start
  96.6 1.4 %copy.12 = f32[64,128]{1,0:T(8,128)} copy(f32[64,128]{1,0:T(8,128)} %get-tuple-element.4) | data formatting | bytes 65536
  98.0 0.0 copy-done
  98.0 0.6 copy.13
Async XLA Ops:
  96.6 1.4 %copy-start = (f32[64,128]{1,0:T(8,128)S(1)}, f32[64,128]{1,0:T(8,128)}, u32[]{:S(2)}) copy-start(f32[64,128]{1,0:T(8,128)} %get-tuple-element.5) | copy-start | bytes 98308
where the time goes:
time: 98.8 us; the launch traced here: 98.6 us
  Pallas kernels  94.7 us (96%)
  local copies, waits for them, and re-layouts  3.28 us (3%)
    pallas_call x1, Pallas kernels, align_all(): pl.pallas_call(body, out_shape=[jax.ShapeDtypeStruct((blk, d), F32)] * 2,...  94.7 us
    unnamed x4, local copies, waits for them, and re-layouts  2 us

commit v1 on v0

v1 whole, which is shorter than its diff:
```python
import functools
import math

import jax
import jax.numpy as jnp
from jax import lax
from jax.experimental import pallas as pl
from jax.experimental.pallas import tpu as pltpu
from jax.sharding import PartitionSpec as P

MESH = pl.DeviceIdType.MESH
F32, BF16 = jnp.float32, jnp.bfloat16
HIGH = lax.Precision.HIGHEST
LOG2E = math.log2(math.e)
NT = (((1,), (1,)), ((), ()))


def dot(a, b, dims=(((1,), (0,)), ((), ()))):
    return lax.dot_general(a, b, dims, preferred_element_type=F32)


def high(a, b, dims=(((1,), (0,)), ((), ()))):
    return lax.dot_general(a, b, dims, precision=HIGH, preferred_element_type=F32)


def split2(v):
    top = v.astype(BF16)
    return top, (v - top.astype(F32)).astype(BF16)


def split3(v):
    top = v.astype(BF16)
    rest = v - top.astype(F32)
    mid = rest.astype(BF16)
    return top, mid, (rest - mid.astype(F32)).astype(BF16)


def eye(rows, shift=0):
    r = lax.broadcasted_iota(jnp.int32, (rows, 128), 0)
    c = lax.broadcasted_iota(jnp.int32, (rows, 128), 1)
    return c == r + shift


def to_lanes(column, mask):
    spread = jnp.broadcast_to(column, mask.shape)
    return jnp.sum(jnp.where(mask, spread, 0.0), axis=0, keepdims=True)


def to_rows(line, mask):
    spread = jnp.broadcast_to(line, mask.shape)
    return jnp.sum(jnp.where(mask, spread, 0.0), axis=1, keepdims=True)


def kernel(
    dims, total, x_ref, y_ref, wq_h, wk_h, gain_h, up_h, bias_h, down_h, out,
    A, B, S, E, MH, ML, T1, T2, K1, K2, K3, AF, AT, BC, RM, RS, RB, RW, CW,
    rsend, csend, rgot, cgot, PS, PR, QS, QX, QR,
    wq, wk, gain, up, bias, down,
    sl, sa, ra_, sb, rb_, rf, ssr, rsr, ssc, rsc, sp, rp, sx, rx, sq, rq,
):
    nx, ny, nz = dims
    row, col = lax.axis_index("row"), lax.axis_index("col")
    x, zl, k = lax.div(row, 4), lax.rem(lax.div(row, 2), 2), lax.rem(row, 2)
    zh, y = lax.div(col, ny), lax.rem(col, ny)
    z = zh * 2 + zl
    me_a, me_b = x * ny + y, z * 2 + k
    blk = x_ref.shape[0]
    rows, cols = nx * ny * blk, nz * 2 * blk
    rchunk, cchunk, schunk = ny * blk, 256, min(512, rows)
    lanes = cchunk // 128
    offset = 0.05 / total
    factor = 2.0 / math.sqrt(x_ref.shape[1]) * LOG2E
    pad = PS.shape[1]
    scope = jax.named_scope

    def at(x, y, z, k):
        return (x * 4 + lax.rem(z, 2) * 2 + k, lax.div(z, 2) * ny + y)

    def plane(n):
        px, py = lax.rem(x + n[0], nx), lax.rem(y + n[1], ny)
        return px * ny + py, at(px, py, z, k)

    def line(dz, other):
        pz = lax.rem(z + dz, nz)
        pk = 1 - k if other else k
        return pz * 2 + pk, at(x, y, pz, pk)

    near = lambda d, n: min(d, n - d)
    plane_steps = sorted(
        [(dx, dy) for dx in range(nx) for dy in range(ny) if (dx, dy) != (0, 0)],
        key=lambda s: -near(s[0], nx) - near(s[1], ny),
    )
    z_steps = sorted(range(1, nz), key=lambda d: near(d, nz))
    line_steps = [(d, o) for d in [*z_steps[::-1], 0] for o in (False, True) if (d, o) != (0, False)]
    _, sibling = line(0, True)

    def copy(src, dst, ss, rs, dev):
        return pltpu.make_async_remote_copy(
            src_ref=src, dst_ref=dst, send_sem=ss, recv_sem=rs, device_id=dev, device_id_type=MESH
        )

    def slot(n):
        return pl.ds(pl.multiple_of(n * blk, blk), blk)

    def chunk(n, size):
        return pl.ds(pl.multiple_of(n * size, size), size)

    with scope("entry"):
        barrier = pltpu.get_barrier_semaphore()
        for step in plane_steps:
            pl.semaphore_signal(barrier, inc=1, device_id=plane(step)[1], device_id_type=MESH)
        for step in line_steps:
            pl.semaphore_signal(barrier, inc=1, device_id=line(*step)[1], device_id_type=MESH)
        moves = [
            (x_ref, A.at[0, slot(me_a)]), (y_ref, B.at[0, slot(me_b)]), (wq_h, wq), (wk_h, wk),
            (gain_h, gain), (up_h, up), (bias_h, bias), (down_h, down),
        ]
        moves = [pltpu.make_async_copy(a, b, sl.at[n]) for n, (a, b) in enumerate(moves)]
        for m in moves:
            m.start()
        for m in moves[:2]:
            m.wait()
        pl.semaphore_wait(barrier, len(plane_steps) + len(line_steps))

    same, small = eye(128), eye(blk)

    def layer(l, carry):
        def send(src, dst, ss, rs, dev):
            copy(src, dst, ss.at[l], rs, dev).start()

        def whole(ref, ss, rs):
            return copy(ref, ref, ss.at[l], rs, sibling)

        own_a, own_b = A.at[l, slot(me_a)], B.at[l, slot(me_b)]
        send(own_b, own_b, sb, rf.at[l], sibling)
        for n, d in enumerate(z_steps[::-1]):
            send(own_b, own_b, sb, rb_.at[l, z], line(d, False)[1])
        for n, step in enumerate(plane_steps):
            send(own_a, own_a, sa, ra_.at[l], plane(step)[1])

        @pl.when(l == 0)
        def _():
            for m in moves[2:]:
                m.wait()

        mix = high(wk[l], wq[l], NT) * factor

        def make_keys(at_):
            k1, k2, k3 = split3(high(B[l, at_, :], mix))
            K1[at_, 0:128] = k1
            K1[at_, 128:256] = k2
            K2[at_, 0:128] = k2
            K2[at_, 128:256] = k1
            K3[at_, 0:128] = k3
            K3[at_, 128:256] = k1

        def make_rows(at_):
            a1, a2, a3 = split3(A[l, at_, :])
            T1[at_, 0:128] = a1
            T1[at_, 128:256] = a2
            T2[at_, 0:128] = a1
            T2[at_, 128:256] = a3

        with scope("gather"):
            for d in z_steps[::-1]:
                s, _ = line(d, False)
                ref, pz = B.at[l, slot(s)], lax.rem(z + d, nz)
                whole(ref, sb, rb_.at[l, pz]).wait_recv()
                send(ref, ref, sb, rf.at[l], sibling)
            whole(A.at[l, pl.ds(0, rows - blk)], sa, ra_.at[l]).wait_recv()
            whole(B.at[l, pl.ds(0, cols // 2)], sb, rf.at[l]).wait_recv()
        with scope("operands"):
            for n in range(cols // 256):
                make_keys(pl.ds(n * 256, 256))
            for n in range(rows // 256):
                make_rows(pl.ds(n * 256, 256))

        def product(n):
            at_ = pl.ds(n * schunk, schunk)
            t1, t2 = T1[at_, :], T2[at_, :]
            S[at_, :] = dot(t1, K1[...], NT) + dot(t1, K2[...], NT) + dot(t2, K3[...], NT)

        def statistics(n, cm, cs):
            base = n * schunk
            new = cm
            for i in range(0, schunk, 8):
                new = jnp.maximum(new, S[base + i : base + i + 8, :])
            cs = cs * jnp.exp2(cm - new)
            for i in range(0, schunk, 8):
                r = pl.ds(base + i, 8)
                s = S[r, :]
                parts = [s[:, j * 128 : (j + 1) * 128] for j in range(cols // 128)]
                m = functools.reduce(jnp.maximum, parts)
                RM[r, :] = m
                RS[r, :] = functools.reduce(jnp.add, [jnp.exp2(p - m) for p in parts])
                cs = cs + jnp.exp2(s - new)
            return new, cs

        def row_lse(n):
            at_ = pl.ds(n * 128, 128)
            m = RM[at_, :]
            p = jnp.max(m, axis=1, keepdims=True)
            t = jnp.sum(RS[at_, :] * jnp.exp2(m - p), axis=1, keepdims=True)
            own = jnp.broadcast_to(p + jnp.log(t) * LOG2E, (128, 128))
            RB[at_, :] = own
            rsend[n : n + 1, :] = to_lanes(own, same)

        with scope("score"):
            cm, cs = jnp.full((8, cols), -jnp.inf, F32), jnp.zeros((8, cols), F32)
            product(0)
            for n in range(rows // schunk):
                if n + 1 < rows // schunk:
                    product(n + 1)
                cm, cs = statistics(n, cm, cs)
        with scope("lse"):
            cpeak = jnp.max(cm, axis=0, keepdims=True)
            clse = cpeak + jnp.log(jnp.sum(cs * jnp.exp2(cm - cpeak), axis=0, keepdims=True)) * LOG2E
            for j in range(cols // 128):
                csend[j : j + 1, :] = clse[:, j * 128 : (j + 1) * 128]
            for n, step in enumerate(line_steps):
                send(csend, cgot.at[l, me_b], ssc, rsc.at[l], line(*step)[1])
            for n in range(rows // 128):
                row_lse(n)
            for n, step in enumerate(plane_steps):
                send(rsend, rgot.at[l, me_a], ssr, rsr.at[l], plane(step)[1])
        cgot[l, me_b] = csend[...]
        rgot[l, me_a] = rsend[...]
        turns = {4: (2, 1, 3, 0), 2: (1, 0), 1: (0,)}
        cturn, rturn = turns[cols // cchunk], turns[rows // rchunk]

        def column_line(ref, b):
            return jnp.concatenate([ref[pl.ds(b * lanes + j, 1), :] for j in range(lanes)], axis=1)

        def matches(n):
            b = lax.rem(zh + cturn[n], len(cturn))
            at_ = chunk(b, cchunk)
            cb = jnp.broadcast_to(column_line(csend, b), (16, cchunk))
            for i in range(0, rows, 16):
                r = pl.ds(i, 16)
                s = S[r, at_]
                rb = RB[r, :]
                m = jnp.exp2((s - jnp.concatenate([rb] * lanes, axis=1)) + (s - cb))
                E[n, r, :] = m
                h, lo = split2(m)
                MH[n, r, :] = h
                ML[n, r, :] = lo

        with scope("match"):
            for n in range(rows // 128):
                AF[:, n * 128 : (n + 1) * 128] = A[l, n * 128 : (n + 1) * 128, :].T
            for n in range(len(cturn)):
                matches(n)

        def lse(got):
            p = jnp.max(got, axis=0)
            return p + jnp.log(jnp.sum(jnp.exp2(got - p), axis=0)) * LOG2E

        with scope("wait_stats"):
            whole(cgot.at[l, pl.ds(0, 2 * nz - 1)], ssc, rsc.at[l]).wait_recv()
            whole(rgot.at[l, pl.ds(0, nx * ny - 1)], ssr, rsr.at[l]).wait_recv()
        with scope("spread"):
            CW[...] = jnp.exp2(csend[...] - lse(cgot[l]))
            RW[...] = jnp.exp2(rsend[...] - lse(rgot[l]))
            for n, turn in enumerate(cturn):
                b = lax.rem(zh + turn, len(cturn))
                for j in range(lanes):
                    w = to_rows(CW[pl.ds(b * lanes + j, 1), :], same)
                    b1, b2 = split2(B[l, chunk(b * lanes + j, 128), :] * w)
                    BC[n, j * 128 : (j + 1) * 128, 0:128] = b1
                    BC[n, j * 128 : (j + 1) * 128, 128:256] = b2
            first = lax.broadcasted_iota(jnp.int32, (16, 128), 0)
            for n in range(rows // 128):
                cut = pl.ds(n * 128, 128)
                v = RW[n : n + 1, :]
                t1, t2 = split2(AF[:, cut] * v)
                AT[0:128, cut] = t2
                AT[128:256, cut] = t1
                low = v - v.astype(BF16).astype(F32)
                AT[256:272, cut] = jnp.where(
                    first == 0, v, jnp.where(first == 1, low, 0.0)
                ).astype(BF16)
                RB[cut, :] = jnp.broadcast_to(to_rows(v, same), (128, 128))

        def to_second(n):
            q = dot(AT[...], MH[n])
            u = dot(AT[128:272, :], ML[n])
            b = lax.rem(zh + cturn[n], len(cturn))
            w = column_line(CW, b)
            mass = (q[256:257] + q[257:258] + u[128:129] + u[129:130]) * w
            q = (q[0:128] + q[128:256] + u[0:128]) * w
            for j in range(lanes):
                t = q[:, j * 128 : (j + 1) * 128].T
                for e in range(2):
                    QS[(b * lanes + j) * 2 + e, 0:blk, :] = t[e * blk : (e + 1) * blk]
                    QS[(b * lanes + j) * 2 + e, blk:pad, :] = jnp.broadcast_to(
                        mass[:, j * 128 : (j + 1) * 128], (pad - blk, 128)
                    )

        def turned(n):
            return lax.rem(zh + cturn[n], len(cturn))

        def cross(n):
            for j in range(lanes):
                pz = turned(n) * lanes + j
                send(QS.at[pz * 2 + (1 - k)], QX.at[l, pz], sx, rx.at[l, turned(n)], sibling)

        def join(n):
            b = turned(n)
            whole(QX.at[l, pl.ds(b * lanes, lanes)], sx, rx.at[l, b]).wait_recv()
            for pz in [b * lanes, b * lanes + 1] if cturn[n] else [b * lanes + 1 - zl]:
                QS[pz * 2 + k] = QS[pz * 2 + k] + QX[l, pz]
                send(QS.at[pz * 2 + k], QR.at[l, z], sq, rq.at[l], at(x, y, pz, k))
            if not cturn[n]:
                QR[l, z] = QS[z * 2 + k] + QX[l, z]

        def to_first(n):
            at_ = chunk(lax.rem(x + rturn[n], len(rturn)), rchunk)
            b = lax.rem(x + rturn[n], len(rturn))
            p = sum(dot(MH[j, at_, :], BC[j]) for j in range(len(cturn)))
            p = p[:, 0:128] + p[:, 128:256]
            p = p + sum(dot(ML[j, at_, :], BC[j, :, 0:128]) for j in range(len(cturn)))
            p = p * RB[at_, :]
            for i in range(0, rchunk, 64):
                r = chunk(b * (rchunk // 64) + i // 64, 64)
                parts = []
                for j, turn in enumerate(cturn):
                    w = column_line(CW, lax.rem(zh + turn, len(cturn)))
                    e = E[j, r, :] * w
                    parts += [e[:, m * 128 : (m + 1) * 128] for m in range(lanes)]
                RM[r, :] = functools.reduce(jnp.add, parts) * RB[r, :]
            mass = jnp.sum(RM[at_, :], axis=1, keepdims=True)
            for e in range(ny):
                PS[b * ny + e, 0:blk, :] = p[e * blk : (e + 1) * blk]
                PS[b * ny + e, blk:pad, :] = jnp.broadcast_to(
                    to_lanes(mass[e * blk : (e + 1) * blk], small), (pad - blk, 128)
                )

        with scope("messages"):
            for n in range(max(len(cturn), len(rturn))):
                if n < len(cturn):
                    with scope("second"):
                        to_second(n)
                    cross(n)
                if n < len(rturn):
                    with scope("first"):
                        to_first(n)
                    for dy in range(ny - 1, -1, -1):
                        if (rturn[n], dy) != (0, 0):
                            s, dev = plane((rturn[n], dy))
                            send(PS.at[s], PR.at[l, me_a], sp, rp.at[l], dev)
                if n < len(cturn):
                    with scope("join"):
                        join(n)
            PR[l, me_a] = PS[me_a]

        with scope("wait_q"):
            whole(QR.at[l, pl.ds(0, nz - 1)], sq, rq.at[l]).wait_recv()
        q = jnp.sum(QR[l], axis=0)
        qm = to_rows(q[blk : blk + 1], eye(blk, lax.rem(me_b, 2) * blk))
        hy = B[l, slot(me_b), :] + q[0:blk] / (qm + offset)
        with scope("wait_p"):
            whole(PR.at[l, pl.ds(0, nx * ny - 1)], sp, rp.at[l]).wait_recv()
        with scope("refine"):
            p = jnp.sum(PR[l], axis=0)
            pm = to_rows(p[blk : blk + 1], small)
            hx = A[l, slot(me_a), :] + p[0:blk] / (pm + offset)
            h = jnp.concatenate([hx, hy], axis=0)
            scale = lax.rsqrt(jnp.mean(h * h, axis=1, keepdims=True) + 1e-05)
            u = high(h * scale * gain[pl.ds(l, 1), :], up[l]) + bias[pl.ds(l, 1), :]
            g = 0.5 * u * (1.0 + jnp.tanh(math.sqrt(2 / math.pi) * (u + 0.044715 * (u * u * u))))
            h = h + high(g, down[l])
            A[l + 1, slot(me_a), :] = h[0:blk]
            B[l + 1, slot(me_b), :] = h[blk : 2 * blk]
        with scope("drain"):
            for ref, s in [
                (A.at[l, pl.ds(0, rows - blk)], sa), (B.at[l, pl.ds(0, cols - blk)], sb),
                (cgot.at[l, pl.ds(0, 2 * nz - 1)], ssc), (rgot.at[l, pl.ds(0, nx * ny - 1)], ssr),
                (PR.at[l, pl.ds(0, nx * ny - 1)], sp), (QX.at[l], sx), (QR.at[l, pl.ds(0, nz - 1)], sq),
            ]:
                whole(ref, s, rq.at[l]).wait_send()
        return carry

    L = wq.shape[0]
    lax.fori_loop(0, L, layer, 0)
    with scope("exit"):
        last = [
            pltpu.make_async_copy(A.at[L, slot(me_a)], out.at[0], sl.at[0]),
            pltpu.make_async_copy(B.at[L, slot(me_b)], out.at[1], sl.at[1]),
        ]
        for c in last:
            c.start()
        for c in last:
            c.wait()


def align_all(dims, x, y, *weights):
    nx, ny, nz = dims
    ga, gb = nx * ny, nz * 2
    blk, d = x.shape
    rows, cols = ga * blk, gb * blk
    L = weights[0].shape[0]
    pad = blk + 8
    V, dma = pltpu.VMEM, lambda *s: pltpu.SemaphoreType.DMA(s)
    body = functools.partial(kernel, dims, blk * ga * gb)
    h = pl.pallas_call(
        body,
        out_shape=jax.ShapeDtypeStruct((2, blk, d), F32),
        in_specs=[pl.BlockSpec(memory_space=pl.ANY)] * 8,
        out_specs=pl.BlockSpec(memory_space=pl.ANY),
        scratch_shapes=[
            V((L + 1, rows, d), F32), V((L + 1, cols, d), F32), V((rows, cols), F32), V((cols // 256, rows, 256), F32),
            V((cols // 256, rows, 256), BF16), V((cols // 256, rows, 256), BF16),
            V((rows, 2 * d), BF16), V((rows, 2 * d), BF16),
            V((cols, 2 * d), BF16), V((cols, 2 * d), BF16), V((cols, 2 * d), BF16),
            V((d, rows), F32), V((2 * d + 16, rows), BF16), V((cols // 256, 256, 2 * d), BF16),
            V((rows, 128), F32), V((rows, 128), F32), V((rows, 128), F32),
            V((rows // 128, 128), F32), V((cols // 128, 128), F32),
            V((rows // 128, 128), F32), V((cols // 128, 128), F32),
            V((L, ga, rows // 128, 128), F32), V((L, gb, cols // 128, 128), F32),
            V((ga, pad, d), F32), V((L, ga, pad, d), F32),
            V((gb, pad, d), F32), V((L, nz, pad, d), F32), V((L, nz, pad, d), F32),
            *[V(w.shape, F32) for w in weights],
            dma(8), dma(L), dma(L), dma(L), dma(L, nz), *[dma(L)] * 8, dma(L, cols // 256), dma(L), dma(L),
        ],
        compiler_params=pltpu.CompilerParams(
            collective_id=0, has_side_effects=True, vmem_limit_bytes=66_000_000
        ),
    )(x, y, *weights)
    return h[0], h[1]


def solution(mesh):
    size = mesh.shape["row"] * mesh.shape["col"]
    dims = (4, 4, 8) if size == 256 else (2, 2, 2)
    placed = (P(("row", "col"), None), P(("row", "col"), None), P(), P(), P(), P(), P(), P())
    return jax.shard_map(
        functools.partial(align_all, dims),
        mesh=mesh,
        in_specs=placed,
        out_specs=(P(("row", "col"), None), P(("row", "col"), None)),
        check_vma=False,
    )
```

time: 98.8 us -> 75.5 us (0.76)
  Pallas kernels: 94.7 us -> 73.3 us
  local copies, waits for them, and re-layouts: 3.28 us -> 1.4 us
    pallas_call x1, Pallas kernels: 94.7 us -> 73.3 us  [align_all(): pl.pallas_call(body, out_shape=jax.ShapeDtypeStruct((2, blk, d), F32), in...]
    unnamed x4 -> x0, local copies, waits for them, and re-layouts: 2 us -> none
    squeeze x0 -> x1, local copies, waits for them, and re-layouts: none -> 1.4 us  [align_all(): return (h[0], h[1])]
    broadcast_in_dim x1 -> x0, local copies, waits for them, and re-layouts: 1.28 us -> none  [align_all(): bias[:, None, :]]
where the time goes in v1:
time: 75.5 us; the launch traced here: 75.3 us
  Pallas kernels  73.3 us (97%)
  local copies, waits for them, and re-layouts  1.4 us (2%)
    pallas_call x1, Pallas kernels, align_all(): pl.pallas_call(body, out_shape=jax.ShapeDtypeStruct((2, blk, d), F32), in...  73.3 us

profile of v1, /device:TPU:1, one launch (start us, length us, event | category | flops | bytes accessed | tf_op | source)
XLA Modules:
  0.0 75.3 jit_solution(2923893192047876632)
XLA Ops:
  0.6 73.3 %shard_map.95 = f32[2,64,128]{2,1,0:T(8,128)} custom-call(f32[64,128]{1,0:T(8,128)} %x_ref.1, f32[64,128]{1,0:T(8,128)} %y_ref.1, f32[2,128,128]{2,1,0:T(8,128)} %wq_h.1, f32[2,128,128]{2,1,0:T(8,128)} %wk_h.1, f32[2,128]{1,0:T(2,128)} %gain_h.1, f32[2,128,512]{2,1,0:T(8,128)} %up_h.1, f32[2,512]{1,0:T(2,128)} %bias_h.1, f32[2,512,128]{2,1,0:T(8,128)} %down_h.1), custom_call_target="tpu_custom_call" | custom-call | tf_op jit(solution)/shard_map/pallas_call | solution.py:405
  73.9 1.4 %slice_bitcast_fusion = (f32[64,128]{1,0:T(8,128)}, f32[64,128]{1,0:T(8,128)}) fusion(f32[2,64,128]{2,1,0:T(8,128)} %shard_map.95), kind=kLoop, calls=%fused_computation | loop fusion | bytes 131072 | tf_op jit(solution)/shard_map/squeeze | solution.py:429

commit v2 on v1

--- a/solution.py
+++ b/solution.py
@@ -66,11 +66,10 @@
     me_a, me_b = x * ny + y, z * 2 + k
     blk = x_ref.shape[0]
     rows, cols = nx * ny * blk, nz * 2 * blk
-    rchunk, cchunk, schunk = ny * blk, 256, min(512, rows)
+    cchunk, schunk = 256, min(256, rows)
     lanes = cchunk // 128
     offset = 0.05 / total
     factor = 2.0 / math.sqrt(x_ref.shape[1]) * LOG2E
-    pad = PS.shape[1]
     scope = jax.named_scope
 
     def at(x, y, z, k):
@@ -143,10 +142,16 @@
             for m in moves[2:]:
                 m.wait()
 
-        mix = high(wk[l], wq[l], NT) * factor
+        m1, m2, m3 = split3(high(wk[l], wq[l], NT) * factor)
+        stack = lambda a, b: jnp.concatenate([a, b], axis=0)
+        mix_a = jnp.concatenate([stack(m1, m2), stack(m2, m1)], axis=1)
+        mix_b = stack(m3, m1)
 
         def make_keys(at_):
-            k1, k2, k3 = split3(high(B[l, at_, :], mix))
+            b1, b2, b3 = split3(B[l, at_, :])
+            t = dot(jnp.concatenate([b1, b2], axis=1), mix_a)
+            t = t[:, 0:128] + (t[:, 128:256] + dot(jnp.concatenate([b1, b3], axis=1), mix_b))
+            k1, k2, k3 = split3(t)
             K1[at_, 0:128] = k1
             K1[at_, 128:256] = k2
             K2[at_, 0:128] = k2
@@ -180,53 +185,61 @@
             t1, t2 = T1[at_, :], T2[at_, :]
             S[at_, :] = dot(t1, K1[...], NT) + dot(t1, K2[...], NT) + dot(t2, K3[...], NT)
 
-        def statistics(n, cm, cs):
-            base = n * schunk
-            new = cm
-            for i in range(0, schunk, 8):
-                new = jnp.maximum(new, S[base + i : base + i + 8, :])
-            cs = cs * jnp.exp2(cm - new)
-            for i in range(0, schunk, 8):
-                r = pl.ds(base + i, 8)
-                s = S[r, :]
-                parts = [s[:, j * 128 : (j + 1) * 128] for j in range(cols // 128)]
+        def row_statistics(n):
+            for i in range(n * schunk, (n + 1) * schunk, 8):
+                r = pl.ds(i, 8)
+                parts = [S[r, j * 128 : (j + 1) * 128] for j in range(cols // 128)]
                 m = functools.reduce(jnp.maximum, parts)
                 RM[r, :] = m
                 RS[r, :] = functools.reduce(jnp.add, [jnp.exp2(p - m) for p in parts])
-                cs = cs + jnp.exp2(s - new)
-            return new, cs
-
-        def row_lse(n):
-            at_ = pl.ds(n * 128, 128)
-            m = RM[at_, :]
-            p = jnp.max(m, axis=1, keepdims=True)
-            t = jnp.sum(RS[at_, :] * jnp.exp2(m - p), axis=1, keepdims=True)
-            own = jnp.broadcast_to(p + jnp.log(t) * LOG2E, (128, 128))
-            RB[at_, :] = own
-            rsend[n : n + 1, :] = to_lanes(own, same)
+            for i in range(n * schunk, (n + 1) * schunk, 128):
+                at_ = pl.ds(i, 128)
+                m = RM[at_, :]
+                p = jnp.max(m, axis=1, keepdims=True)
+                t = jnp.sum(RS[at_, :] * jnp.exp2(m - p), axis=1, keepdims=True)
+                own = jnp.broadcast_to(p + jnp.log(t) * LOG2E, (128, 128))
+                RB[at_, :] = own
+                rsend[i // 128 : i // 128 + 1, :] = to_lanes(own, same)
+
+        def column_statistics(j):
+            at_ = pl.ds(j * cchunk, cchunk)
+            m = [S[i * 8 : (i + 1) * 8, at_] for i in range(4)]
+            for i in range(32, rows, 32):
+                m = [jnp.maximum(m[e], S[i + e * 8 : i + e * 8 + 8, at_]) for e in range(4)]
+            p = jnp.max(functools.reduce(jnp.maximum, m), axis=0, keepdims=True)
+            pb = jnp.broadcast_to(p, (8, cchunk))
+            t = [jnp.zeros((8, cchunk), F32)] * 4
+            for i in range(0, rows, 32):
+                t = [t[e] + jnp.exp2(S[i + e * 8 : i + e * 8 + 8, at_] - pb) for e in range(4)]
+            c = p + jnp.log(jnp.sum(functools.reduce(jnp.add, t), axis=0, keepdims=True)) * LOG2E
+            for e in range(lanes):
+                csend[j * lanes + e : j * lanes + e + 1, :] = c[:, e * 128 : (e + 1) * 128]
 
         with scope("score"):
-            cm, cs = jnp.full((8, cols), -jnp.inf, F32), jnp.zeros((8, cols), F32)
             product(0)
             for n in range(rows // schunk):
                 if n + 1 < rows // schunk:
                     product(n + 1)
-                cm, cs = statistics(n, cm, cs)
+                row_statistics(n)
+            for n, step in enumerate(plane_steps):
+                send(rsend, rgot.at[l, me_a], ssr, rsr.at[l], plane(step)[1])
         with scope("lse"):
-            cpeak = jnp.max(cm, axis=0, keepdims=True)
-            clse = cpeak + jnp.log(jnp.sum(cs * jnp.exp2(cm - cpeak), axis=0, keepdims=True)) * LOG2E
-            for j in range(cols // 128):
-                csend[j : j + 1, :] = clse[:, j * 128 : (j + 1) * 128]
+            for j in range(cols // cchunk):
+                column_statistics(j)
             for n, step in enumerate(line_steps):
                 send(csend, cgot.at[l, me_b], ssc, rsc.at[l], line(*step)[1])
-            for n in range(rows // 128):
-                row_lse(n)
-            for n, step in enumerate(plane_steps):
-                send(rsend, rgot.at[l, me_a], ssr, rsr.at[l], plane(step)[1])
         cgot[l, me_b] = csend[...]
         rgot[l, me_a] = rsend[...]
         turns = {4: (2, 1, 3, 0), 2: (1, 0), 1: (0,)}
-        cturn, rturn = turns[cols // cchunk], turns[rows // rchunk]
+        cturn = turns[cols // cchunk]
+        parcels = {
+            4: [
+                [(2, 2), (2, 0), (0, 2), (1, 1)], [(1, 2), (3, 2), (2, 1), (2, 3)],
+                [(1, 3), (3, 1), (3, 3), (1, 0)], [(3, 0), (0, 1), (0, 3), (0, 0)],
+            ],
+            2: [[(1, 1), (1, 0), (0, 1), (0, 0)]],
+        }[nx]
+        body = pl.ds(0, blk + 1)
 
         def column_line(ref, b):
             return jnp.concatenate([ref[pl.ds(b * lanes + j, 1), :] for j in range(lanes)], axis=1)
@@ -255,19 +268,10 @@
             p = jnp.max(got, axis=0)
             return p + jnp.log(jnp.sum(jnp.exp2(got - p), axis=0)) * LOG2E
 
-        with scope("wait_stats"):
-            whole(cgot.at[l, pl.ds(0, 2 * nz - 1)], ssc, rsc.at[l]).wait_recv()
+        with scope("wait_rows"):
             whole(rgot.at[l, pl.ds(0, nx * ny - 1)], ssr, rsr.at[l]).wait_recv()
         with scope("spread"):
-            CW[...] = jnp.exp2(csend[...] - lse(cgot[l]))
             RW[...] = jnp.exp2(rsend[...] - lse(rgot[l]))
-            for n, turn in enumerate(cturn):
-                b = lax.rem(zh + turn, len(cturn))
-                for j in range(lanes):
-                    w = to_rows(CW[pl.ds(b * lanes + j, 1), :], same)
-                    b1, b2 = split2(B[l, chunk(b * lanes + j, 128), :] * w)
-                    BC[n, j * 128 : (j + 1) * 128, 0:128] = b1
-                    BC[n, j * 128 : (j + 1) * 128, 128:256] = b2
             first = lax.broadcasted_iota(jnp.int32, (16, 128), 0)
             for n in range(rows // 128):
                 cut = pl.ds(n * 128, 128)
@@ -279,11 +283,31 @@
                 AT[256:272, cut] = jnp.where(
                     first == 0, v, jnp.where(first == 1, low, 0.0)
                 ).astype(BF16)
-                RB[cut, :] = jnp.broadcast_to(to_rows(v, same), (128, 128))
+
+        def column_weights():
+            with scope("wait_columns"):
+                whole(cgot.at[l, pl.ds(0, 2 * nz - 1)], ssc, rsc.at[l]).wait_recv()
+            CW[...] = jnp.exp2(csend[...] - lse(cgot[l]))
+
+        def first_operands():
+            with scope("spread"):
+                for n, turn in enumerate(cturn):
+                    b = lax.rem(zh + turn, len(cturn))
+                    for j in range(lanes):
+                        w = to_rows(CW[pl.ds(b * lanes + j, 1), :], same)
+                        b1, b2 = split2(B[l, chunk(b * lanes + j, 128), :] * w)
+                        BC[n, j * 128 : (j + 1) * 128, 0:128] = b1
+                        BC[n, j * 128 : (j + 1) * 128, 128:256] = b2
+                for n in range(rows // 128):
+                    RB[n * 128 : (n + 1) * 128, :] = jnp.broadcast_to(
+                        to_rows(RW[n : n + 1, :], same), (128, 128)
+                    )
 
         def to_second(n):
             q = dot(AT[...], MH[n])
             u = dot(AT[128:272, :], ML[n])
+            if n == 0:
+                column_weights()
             b = lax.rem(zh + cturn[n], len(cturn))
             w = column_line(CW, b)
             mass = (q[256:257] + q[257:258] + u[128:129] + u[129:130]) * w
@@ -292,9 +316,7 @@
                 t = q[:, j * 128 : (j + 1) * 128].T
                 for e in range(2):
                     QS[(b * lanes + j) * 2 + e, 0:blk, :] = t[e * blk : (e + 1) * blk]
-                    QS[(b * lanes + j) * 2 + e, blk:pad, :] = jnp.broadcast_to(
-                        mass[:, j * 128 : (j + 1) * 128], (pad - blk, 128)
-                    )
+                    QS[(b * lanes + j) * 2 + e, blk : blk + 1, :] = mass[:, j * 128 : (j + 1) * 128]
 
         def turned(n):
             return lax.rem(zh + cturn[n], len(cturn))
@@ -302,66 +324,81 @@
         def cross(n):
             for j in range(lanes):
                 pz = turned(n) * lanes + j
-                send(QS.at[pz * 2 + (1 - k)], QX.at[l, pz], sx, rx.at[l, turned(n)], sibling)
+                send(QS.at[pz * 2 + (1 - k), body], QX.at[l, pz, body], sx, rx.at[l, turned(n)], sibling)
 
         def join(n):
             b = turned(n)
-            whole(QX.at[l, pl.ds(b * lanes, lanes)], sx, rx.at[l, b]).wait_recv()
+            whole(QX.at[l, pl.ds(b * lanes, lanes), body], sx, rx.at[l, b]).wait_recv()
             for pz in [b * lanes, b * lanes + 1] if cturn[n] else [b * lanes + 1 - zl]:
-                QS[pz * 2 + k] = QS[pz * 2 + k] + QX[l, pz]
-                send(QS.at[pz * 2 + k], QR.at[l, z], sq, rq.at[l], at(x, y, pz, k))
+                QS[pz * 2 + k, body] = QS[pz * 2 + k, body] + QX[l, pz, body]
+                send(QS.at[pz * 2 + k, body], QR.at[l, z, body], sq, rq.at[l], at(x, y, pz, k))
             if not cturn[n]:
-                QR[l, z] = QS[z * 2 + k] + QX[l, z]
+                QR[l, z, body] = QS[z * 2 + k, body] + QX[l, z, body]
 
         def to_first(n):
-            at_ = chunk(lax.rem(x + rturn[n], len(rturn)), rchunk)
-            b = lax.rem(x + rturn[n], len(rturn))
-            p = sum(dot(MH[j, at_, :], BC[j]) for j in range(len(cturn)))
+            owners = [plane(o)[0] for o in parcels[n]]
+            left = lambda ref: jnp.concatenate([ref[slot(s), :] for s in owners], axis=0)
+            p = sum(dot(left(MH.at[j]), BC[j]) for j in range(len(cturn)))
             p = p[:, 0:128] + p[:, 128:256]
-            p = p + sum(dot(ML[j, at_, :], BC[j, :, 0:128]) for j in range(len(cturn)))
-            p = p * RB[at_, :]
-            for i in range(0, rchunk, 64):
-                r = chunk(b * (rchunk // 64) + i // 64, 64)
+            p = p + sum(dot(left(ML.at[j]), BC[j, :, 0:128]) for j in range(len(cturn)))
+            for e, s in enumerate(owners):
                 parts = []
                 for j, turn in enumerate(cturn):
                     w = column_line(CW, lax.rem(zh + turn, len(cturn)))
-                    e = E[j, r, :] * w
-                    parts += [e[:, m * 128 : (m + 1) * 128] for m in range(lanes)]
-                RM[r, :] = functools.reduce(jnp.add, parts) * RB[r, :]
-            mass = jnp.sum(RM[at_, :], axis=1, keepdims=True)
-            for e in range(ny):
-                PS[b * ny + e, 0:blk, :] = p[e * blk : (e + 1) * blk]
-                PS[b * ny + e, blk:pad, :] = jnp.broadcast_to(
-                    to_lanes(mass[e * blk : (e + 1) * blk], small), (pad - blk, 128)
-                )
+                    t = E[j, slot(s), :] * w
+                    parts += [t[:, m * 128 : (m + 1) * 128] for m in range(lanes)]
+                v = RB[slot(s), :]
+                mass = jnp.sum(functools.reduce(jnp.add, parts) * v, axis=1, keepdims=True)
+                PS[s, 0:blk, :] = p[e * blk : (e + 1) * blk] * v
+                PS[s, blk : blk + 1, :] = to_lanes(mass, small)
+
+        def give(n):
+            to_first(n)
+            for o in parcels[n]:
+                s, dev = plane(o)
+                if o != (0, 0):
+                    send(PS.at[s, body], PR.at[l, me_a, body], sp, rp.at[l], dev)
+                else:
+                    PR[l, me_a, body] = PS[me_a, body]
 
         with scope("messages"):
-            for n in range(max(len(cturn), len(rturn))):
-                if n < len(cturn):
-                    with scope("second"):
-                        to_second(n)
-                    cross(n)
-                if n < len(rturn):
-                    with scope("first"):
-                        to_first(n)
-                    for dy in range(ny - 1, -1, -1):
-                        if (rturn[n], dy) != (0, 0):
-                            s, dev = plane((rturn[n], dy))
-                            send(PS.at[s], PR.at[l, me_a], sp, rp.at[l], dev)
-                if n < len(cturn):
-                    with scope("join"):
-                        join(n)
-            PR[l, me_a] = PS[me_a]
+            def second(n):
+                with scope("second"):
+                    to_second(n)
+                cross(n)
+                if n == 0:
+                    first_operands()
+
+            def first(n):
+                with scope("first"):
+                    give(n)
+
+            def joined(n):
+                with scope("join"):
+                    join(n)
+
+            if len(cturn) == 4:
+                for f, n in zip(
+                    (second, first, joined, second, second, joined, first, second, joined, first, joined, first),
+                    (0, 0, 0, 1, 2, 1, 1, 3, 2, 2, 3, 3),
+                ):
+                    f(n)
+            else:
+                for n in range(len(cturn)):
+                    second(n)
+                    joined(n)
+                for n in range(len(parcels)):
+                    first(n)
 
         with scope("wait_q"):
-            whole(QR.at[l, pl.ds(0, nz - 1)], sq, rq.at[l]).wait_recv()
-        q = jnp.sum(QR[l], axis=0)
+            whole(QR.at[l, pl.ds(0, nz - 1), body], sq, rq.at[l]).wait_recv()
+        q = jnp.sum(QR[l, :, body], axis=0)
         qm = to_rows(q[blk : blk + 1], eye(blk, lax.rem(me_b, 2) * blk))
         hy = B[l, slot(me_b), :] + q[0:blk] / (qm + offset)
         with scope("wait_p"):
-            whole(PR.at[l, pl.ds(0, nx * ny - 1)], sp, rp.at[l]).wait_recv()
+            whole(PR.at[l, pl.ds(0, nx * ny - 1), body], sp, rp.at[l]).wait_recv()
         with scope("refine"):
-            p = jnp.sum(PR[l], axis=0)
+            p = jnp.sum(PR[l, :, body], axis=0)
             pm = to_rows(p[blk : blk + 1], small)
             hx = A[l, slot(me_a), :] + p[0:blk] / (pm + offset)
             h = jnp.concatenate([hx, hy], axis=0)
@@ -375,7 +412,8 @@
             for ref, s in [
                 (A.at[l, pl.ds(0, rows - blk)], sa), (B.at[l, pl.ds(0, cols - blk)], sb),
                 (cgot.at[l, pl.ds(0, 2 * nz - 1)], ssc), (rgot.at[l, pl.ds(0, nx * ny - 1)], ssr),
-                (PR.at[l, pl.ds(0, nx * ny - 1)], sp), (QX.at[l], sx), (QR.at[l, pl.ds(0, nz - 1)], sq),
+                (PR.at[l, pl.ds(0, nx * ny - 1), body], sp), (QX.at[l, :, body], sx),
+                (QR.at[l, pl.ds(0, nz - 1), body], sq),
             ]:
                 whole(ref, s, rq.at[l]).wait_send()
         return carry

time: 75.5 us -> 70.3 us (0.931)
  Pallas kernels: 73.3 us -> 68.1 us
    pallas_call x1, Pallas kernels: 73.3 us -> 68.1 us  [align_all(): pl.pallas_call(body, out_shape=jax.ShapeDtypeStruct((2, blk, d), F32), in...]
where the time goes in v2:
time: 70.3 us; the launch traced here: 70.1 us
  Pallas kernels  68.1 us (97%)
  local copies, waits for them, and re-layouts  1.4 us (2%)
    pallas_call x1, Pallas kernels, align_all(): pl.pallas_call(body, out_shape=jax.ShapeDtypeStruct((2, blk, d), F32), in...  68.1 us

profile of v2, /device:TPU:1, one launch (start us, length us, event | category | flops | bytes accessed | tf_op | source)
XLA Modules:
  0.0 70.1 jit_solution(11959887886101015027)
XLA Ops:
  0.6 68.1 %shard_map.95 = f32[2,64,128]{2,1,0:T(8,128)} custom-call(f32[64,128]{1,0:T(8,128)} %x_ref.1, f32[64,128]{1,0:T(8,128)} %y_ref.1, f32[2,128,128]{2,1,0:T(8,128)} %wq_h.1, f32[2,128,128]{2,1,0:T(8,128)} %wk_h.1, f32[2,128]{1,0:T(2,128)} %gain_h.1, f32[2,128,512]{2,1,0:T(8,128)} %up_h.1, f32[2,512]{1,0:T(2,128)} %bias_h.1, f32[2,512,128]{2,1,0:T(8,128)} %down_h.1), custom_call_target="tpu_custom_call" | custom-call | tf_op jit(solution)/shard_map/pallas_call | solution.py:443
  68.7 1.4 %slice_bitcast_fusion = (f32[64,128]{1,0:T(8,128)}, f32[64,128]{1,0:T(8,128)}) fusion(f32[2,64,128]{2,1,0:T(8,128)} %shard_map.95), kind=kLoop, calls=%fused_computation | loop fusion | bytes 131072 | tf_op jit(solution)/shard_map/squeeze | solution.py:467

commit v3 on v2

--- a/solution.py
+++ b/solution.py
@@ -55,7 +55,7 @@
     dims, total, x_ref, y_ref, wq_h, wk_h, gain_h, up_h, bias_h, down_h, out,
     A, B, S, E, MH, ML, T1, T2, K1, K2, K3, AF, AT, BC, RM, RS, RB, RW, CW,
     rsend, csend, rgot, cgot, PS, PR, QS, QX, QR,
-    wq, wk, gain, up, bias, down,
+    wq, wk, gain, up, bias, down, U, W,
     sl, sa, ra_, sb, rb_, rf, ssr, rsr, ssc, rsc, sp, rp, sx, rx, sq, rq,
 ):
     nx, ny, nz = dims
@@ -167,18 +167,26 @@
             T2[at_, 128:256] = a3
 
         with scope("gather"):
-            for d in z_steps[::-1]:
+            for n, d in enumerate(z_steps[::-1]):
                 s, _ = line(d, False)
                 ref, pz = B.at[l, slot(s)], lax.rem(z + d, nz)
                 whole(ref, sb, rb_.at[l, pz]).wait_recv()
                 send(ref, ref, sb, rf.at[l], sibling)
+                if n == 0:
+                    make_keys(slot(me_b))
+                if n < 2:
+                    make_keys(slot(s))
+            with scope("operands"):
+                for d in z_steps[::-1][2:]:
+                    make_keys(slot(line(d, False)[0]))
             whole(A.at[l, pl.ds(0, rows - blk)], sa, ra_.at[l]).wait_recv()
+            with scope("operands"):
+                for n in range(rows // 256):
+                    make_rows(pl.ds(n * 256, 256))
             whole(B.at[l, pl.ds(0, cols // 2)], sb, rf.at[l]).wait_recv()
-        with scope("operands"):
-            for n in range(cols // 256):
-                make_keys(pl.ds(n * 256, 256))
-            for n in range(rows // 256):
-                make_rows(pl.ds(n * 256, 256))
+            with scope("operands"):
+                for n in range(nz):
+                    make_keys(slot(n * 2 + 1 - k))
 
         def product(n):
             at_ = pl.ds(n * schunk, schunk)
@@ -268,6 +276,15 @@
             p = jnp.max(got, axis=0)
             return p + jnp.log(jnp.sum(jnp.exp2(got - p), axis=0)) * LOG2E
 
+        with scope("weights"):
+            u1, u2 = split2(up[l])
+            U[0, 0:128, :] = u1
+            U[0, 128:256, :] = u1
+            U[1, 0:128, :] = u2
+            U[1, 128:256, :] = u2
+            w1, w2 = split2(down[l])
+            W[:, 0:128] = w1
+            W[:, 128:256] = w2
         with scope("wait_rows"):
             whole(rgot.at[l, pl.ds(0, nx * ny - 1)], ssr, rsr.at[l]).wait_recv()
         with scope("spread"):
@@ -403,9 +420,13 @@
             hx = A[l, slot(me_a), :] + p[0:blk] / (pm + offset)
             h = jnp.concatenate([hx, hy], axis=0)
             scale = lax.rsqrt(jnp.mean(h * h, axis=1, keepdims=True) + 1e-05)
-            u = high(h * scale * gain[pl.ds(l, 1), :], up[l]) + bias[pl.ds(l, 1), :]
+            n1, n2 = split2(h * scale * gain[pl.ds(l, 1), :])
+            n12 = jnp.concatenate([n1, n2], axis=1)
+            u = dot(n12, U[0]) + dot(n12, U[1]) + bias[pl.ds(l, 1), :]
             g = 0.5 * u * (1.0 + jnp.tanh(math.sqrt(2 / math.pi) * (u + 0.044715 * (u * u * u))))
-            h = h + high(g, down[l])
+            g1, g2 = split2(g)
+            t = dot(g1, W[...]) + dot(g2, W[...])
+            h = h + (t[:, 0:128] + t[:, 128:256])
             A[l + 1, slot(me_a), :] = h[0:blk]
             B[l + 1, slot(me_b), :] = h[blk : 2 * blk]
         with scope("drain"):
@@ -458,12 +479,13 @@
             V((ga, pad, d), F32), V((L, ga, pad, d), F32),
             V((gb, pad, d), F32), V((L, nz, pad, d), F32), V((L, nz, pad, d), F32),
             *[V(w.shape, F32) for w in weights],
+            V((2, 2 * d, weights[3].shape[2]), BF16), V((weights[3].shape[2], 2 * d), BF16),
             dma(8), dma(L), dma(L), dma(L), dma(L, nz), *[dma(L)] * 8, dma(L, cols // 256), dma(L), dma(L),
         ],
         compiler_params=pltpu.CompilerParams(
-            collective_id=0, has_side_effects=True, vmem_limit_bytes=66_000_000
+            collective_id=0, has_side_effects=True, vmem_limit_bytes=48 * 1024 * 1024
         ),
-    )(x, y, *weights)
+    )(*[pltpu.with_memory_space_constraint(a, pltpu.MemorySpace.HBM) for a in (x, y, *weights)])
     return h[0], h[1]
 
 

time: 70.3 us -> 68.5 us (0.974)
  Pallas kernels: 68.1 us -> 67.2 us
  local copies, waits for them, and re-layouts: 1.4 us -> 0.63 us
    pallas_call x1, Pallas kernels: 68.1 us -> 67.2 us  [align_all(): pl.pallas_call(body, out_shape=jax.ShapeDtypeStruct((2, blk, d), F32), in...]
    squeeze x1, local copies, waits for them, and re-layouts: 1.4 us -> 0.63 us  [align_all(): return (h[0], h[1])]
where the time goes in v3:
time: 68.5 us; the launch traced here: 68.4 us
  Pallas kernels  67.2 us (98%)
    pallas_call x1, Pallas kernels, align_all(): pl.pallas_call(body, out_shape=jax.ShapeDtypeStruct((2, blk, d), F32), in...  67.2 us

profile of v3, /device:TPU:1, one launch (start us, length us, event | category | flops | bytes accessed | tf_op | source)
XLA Modules:
  0.0 68.4 jit_solution(10352236491249698802)
XLA Ops:
  0.6 67.2 %shard_map.95 = f32[2,64,128]{2,1,0:T(8,128)S(1)} custom-call(f32[64,128]{1,0:T(8,128)} %x_ref.1, f32[64,128]{1,0:T(8,128)} %y_ref.1, f32[2,128,128]{2,1,0:T(8,128)} %wq_h.1, f32[2,128,128]{2,1,0:T(8,128)} %wk_h.1, f32[2,128]{1,0:T(2,128)} %gain_h.1, f32[2,128,512]{2,1,0:T(8,128)} %up_h.1, f32[2,512]{1,0:T(2,128)} %bias_h.1, f32[2,512,128]{2,1,0:T(8,128)} %down_h.1), custom_call_target="tpu_custom_call" | custom-call | tf_op jit(solution)/shard_map/pallas_call | solution.py:464
  67.8 0.6 slice_bitcast_fusion

commit v4 on v3

--- a/solution.py
+++ b/solution.py
@@ -134,7 +134,7 @@
         send(own_b, own_b, sb, rf.at[l], sibling)
         for n, d in enumerate(z_steps[::-1]):
             send(own_b, own_b, sb, rb_.at[l, z], line(d, False)[1])
-        for n, step in enumerate(plane_steps):
+        for n, step in enumerate([(2, 2), (2, 0), (0, 2), (1, 1), (3, 3), (1, 2), (3, 2), (2, 1), (2, 3), (1, 3), (3, 1), (1, 0), (3, 0), (0, 1), (0, 3)]):
             send(own_a, own_a, sa, ra_.at[l], plane(step)[1])
 
         @pl.when(l == 0)
@@ -287,7 +287,7 @@
             W[:, 128:256] = w2
         with scope("wait_rows"):
             whole(rgot.at[l, pl.ds(0, nx * ny - 1)], ssr, rsr.at[l]).wait_recv()
-        with scope("spread"):
+        if True:
             RW[...] = jnp.exp2(rsend[...] - lse(rgot[l]))
             first = lax.broadcasted_iota(jnp.int32, (16, 128), 0)
             for n in range(rows // 128):
@@ -300,6 +300,7 @@
                 AT[256:272, cut] = jnp.where(
                     first == 0, v, jnp.where(first == 1, low, 0.0)
                 ).astype(BF16)
+                RB[cut, :] = jnp.broadcast_to(to_rows(v, same), (128, 128))
 
         def column_weights():
             with scope("wait_columns"):
@@ -315,10 +316,6 @@
                         b1, b2 = split2(B[l, chunk(b * lanes + j, 128), :] * w)
                         BC[n, j * 128 : (j + 1) * 128, 0:128] = b1
                         BC[n, j * 128 : (j + 1) * 128, 128:256] = b2
-                for n in range(rows // 128):
-                    RB[n * 128 : (n + 1) * 128, :] = jnp.broadcast_to(
-                        to_rows(RW[n : n + 1, :], same), (128, 128)
-                    )
 
         def to_second(n):
             q = dot(AT[...], MH[n])
@@ -396,8 +393,8 @@
 
             if len(cturn) == 4:
                 for f, n in zip(
-                    (second, first, joined, second, second, joined, first, second, joined, first, joined, first),
-                    (0, 0, 0, 1, 2, 1, 1, 3, 2, 2, 3, 3),
+                    (second, first, joined, second, first, second, joined, first, joined, second, first, joined),
+                    (0, 0, 0, 1, 1, 2, 1, 2, 2, 3, 3, 3),
                 ):
                     f(n)
             else:

time: 68.5 us -> 67.9 us (level)
  Pallas kernels: 67.2 us -> 66.5 us
where the time goes in v4:
time: 67.9 us; the launch traced here: 67.8 us
  Pallas kernels  66.5 us (98%)
    pallas_call x1, Pallas kernels, align_all(): pl.pallas_call(body, out_shape=jax.ShapeDtypeStruct((2, blk, d), F32), in...  66.5 us

profile of v4, /device:TPU:1, one launch (start us, length us, event | category | flops | bytes accessed | tf_op | source)
XLA Modules:
  0.0 67.8 jit_solution(1698127420476709609)
XLA Ops:
  0.6 66.5 %shard_map.95 = f32[2,64,128]{2,1,0:T(8,128)S(1)} custom-call(f32[64,128]{1,0:T(8,128)} %x_ref.1, f32[64,128]{1,0:T(8,128)} %y_ref.1, f32[2,128,128]{2,1,0:T(8,128)} %wq_h.1, f32[2,128,128]{2,1,0:T(8,128)} %wk_h.1, f32[2,128]{1,0:T(2,128)} %gain_h.1, f32[2,128,512]{2,1,0:T(8,128)} %up_h.1, f32[2,512]{1,0:T(2,128)} %bias_h.1, f32[2,512,128]{2,1,0:T(8,128)} %down_h.1), custom_call_target="tpu_custom_call" | custom-call | tf_op jit(solution)/shard_map/pallas_call | solution.py:461
  67.2 0.6 slice_bitcast_fusion

commit v5 on v4

--- a/solution.py
+++ b/solution.py
@@ -134,6 +134,8 @@
         send(own_b, own_b, sb, rf.at[l], sibling)
         for n, d in enumerate(z_steps[::-1]):
             send(own_b, own_b, sb, rb_.at[l, z], line(d, False)[1])
+            if d in (1, nz - 1):
+                send(own_b, own_b, sb, rf.at[l], line(d, True)[1])
         for n, step in enumerate([(2, 2), (2, 0), (0, 2), (1, 1), (3, 3), (1, 2), (3, 2), (2, 1), (2, 3), (1, 3), (3, 1), (1, 0), (3, 0), (0, 1), (0, 3)]):
             send(own_a, own_a, sa, ra_.at[l], plane(step)[1])
 
@@ -171,7 +173,8 @@
                 s, _ = line(d, False)
                 ref, pz = B.at[l, slot(s)], lax.rem(z + d, nz)
                 whole(ref, sb, rb_.at[l, pz]).wait_recv()
-                send(ref, ref, sb, rf.at[l], sibling)
+                if d not in (1, nz - 1):
+                    send(ref, ref, sb, rf.at[l], sibling)
                 if n == 0:
                     make_keys(slot(me_b))
                 if n < 2:

time: 67.9 us -> 68.2 us (level)
  no operation moved by 1% of the time
where the time goes in v5:
time: 68.2 us; the launch traced here: 68.1 us
  Pallas kernels  66.9 us (98%)
    pallas_call x1, Pallas kernels, align_all(): pl.pallas_call(body, out_shape=jax.ShapeDtypeStruct((2, blk, d), F32), in...  66.9 us

profile of v5, /device:TPU:1, one launch (start us, length us, event | category | flops | bytes accessed | tf_op | source)
XLA Modules:
  0.0 68.1 jit_solution(14393181035438783332)
XLA Ops:
  0.6 66.9 %shard_map.95 = f32[2,64,128]{2,1,0:T(8,128)S(1)} custom-call(f32[64,128]{1,0:T(8,128)} %x_ref.1, f32[64,128]{1,0:T(8,128)} %y_ref.1, f32[2,128,128]{2,1,0:T(8,128)} %wq_h.1, f32[2,128,128]{2,1,0:T(8,128)} %wk_h.1, f32[2,128]{1,0:T(2,128)} %gain_h.1, f32[2,128,512]{2,1,0:T(8,128)} %up_h.1, f32[2,512]{1,0:T(2,128)} %bias_h.1, f32[2,512,128]{2,1,0:T(8,128)} %down_h.1), custom_call_target="tpu_custom_call" | custom-call | tf_op jit(solution)/shard_map/pallas_call | solution.py:464
  67.5 0.6 slice_bitcast_fusion
